TPU v7x, 32 devices: a whole 2x2x4 slice. The times are simulated.
32 devices in a mesh: dom: 16 (over z, y, x), feat: 2 (over core).
Axes of the slice: x: 2, y: 2, z: 4, core: 2. Of those that a mesh axis runs over, the one named last changes fastest.
Arguments:
- features: bfloat16 [32768, 608], P('dom', 'feat'), may hold values from -6 to 6
- weight: bfloat16 [608, 256], replicated, may hold values from -0.25 to 0.25
- out_bias: float32 [256], P('feat'), may hold values from -3 to 3
- tile_values: bfloat16 [1728, 128, 128], P('dom'), may hold values from -0.25 to 0.25
- tile_rows: int32 [1728], P('dom'), may hold values from 0 to 15
- tile_cols: int32 [1728], P('dom'), may hold values from 0 to 81, as said below
- tile_count: int32 [16], P('dom'), may hold values from 10 to 108, as said below
- send_rows: int32 [16, 8, 1024], P('dom'), may hold values from 0 to 2047
- hub_ids: int32 [256], replicated, may hold values from 0 to 32767, as said below
Outputs:
- activations: bfloat16 [32768, 256], P('dom', 'feat')
Inputs may be any that keep to these rules, and one draw needn't show every extreme that they name: `tile_count`: slots at or past a partition's count are not part of the graph; some partition uses all 108 slots. `tile_cols`: column blocks index the extended row space of the slot's partition. `hub_ids`: distinct vertex ids; vertex v belongs to partition v // 2048; no partition owns more than 48 hubs, and some partition owns exactly 48.
All inputs are finite; a program needn't handle non-finite values.
Results may differ from a plain program's by a relative error of at most 0.0044.
Values may be sent and summed in bfloat16 or wider, within the bound.
A program may use at most 64 MiB of HBM per device.

v0:
```python
import functools
import math

import jax
import jax.numpy as jnp
from jax import lax
from jax.experimental import pallas as pl
from jax.experimental.pallas import tpu as pltpu
from jax.sharding import PartitionSpec as P

REACH = 4
HUB_MOST = 48


def passed_along(value, axis, steps):
    count = lax.axis_size(axis)
    initial, last = (max(0, -steps), min(count, count - steps))
    return lax.ppermute(value, axis, [(source, source + steps) for source in range(initial, last)])


def local_any(
    features, weight, out_bias, tile_values, tile_rows, tile_cols, tile_count, send_rows, hub_ids
):
    column_count = out_bias.shape[0]
    vertex_rows = features.shape[0]
    part_index = lax.axis_index("dom")
    feat_index = lax.axis_index("feat")
    weight_cols = lax.dynamic_slice_in_dim(weight, feat_index * column_count, column_count, 1)
    summed = jnp.dot(
        lax.all_gather(features, "feat", axis=1, tiled=True),
        weight_cols,
        preferred_element_type=jnp.float32,
    )
    projected = summed.astype(jnp.bfloat16)
    half_rows = send_rows.shape[2]
    slot_total = send_rows.shape[1]
    offsets = list(range(-REACH, 0)) + list(range(1, REACH + 1))
    packed_all = projected[send_rows[0].reshape(slot_total * half_rows)].reshape(
        slot_total, half_rows, column_count
    )
    received = []
    for slot_index, offset_value in enumerate(offsets):
        received.append(passed_along(packed_all[slot_index], "dom", offset_value))
    halo_block = jnp.concatenate(received, 0)
    owners = hub_ids // vertex_rows
    mine = owners == part_index
    local_index = jnp.clip(hub_ids - part_index * vertex_rows, 0, vertex_rows - 1)
    candidates = projected[local_index]
    hub_total = hub_ids.shape[0]
    positions = jnp.arange(hub_total, dtype=jnp.int32)
    earlier = (owners[:, None] == owners[None, :]) & (positions[:, None] > positions[None, :])
    ranks = jnp.sum(earlier.astype(jnp.int32), 1)
    selector = (
        mine[:, None] & (ranks[:, None] == jnp.arange(HUB_MOST, dtype=jnp.int32)[None, :])
    ).astype(jnp.bfloat16)
    slot_rows = lax.dot_general(
        selector, candidates, (((0,), (0,)), ((), ())), preferred_element_type=jnp.float32
    ).astype(jnp.bfloat16)
    gathered = lax.all_gather(slot_rows, "dom", axis=0, tiled=True)
    hub_block = gathered[owners * HUB_MOST + ranks]
    extended = jnp.concatenate([projected, halo_block, hub_block], 0)
    block_edge = tile_values.shape[1]
    blocks = extended.reshape(extended.shape[0] // block_edge, block_edge, column_count)
    products = jnp.einsum(
        "tij,tjc->tic", tile_values, blocks[tile_cols], preferred_element_type=jnp.float32
    )
    live_mask = jnp.arange(tile_values.shape[0], dtype=jnp.int32) < tile_count[0]
    block_count = vertex_rows // block_edge
    assignment = (
        (tile_rows[None, :] == jnp.arange(block_count, dtype=jnp.int32)[:, None])
        & live_mask[None, :]
    ).astype(jnp.float32)
    aggregate = jnp.einsum("rt,tic->ric", assignment, products, precision=lax.Precision.HIGHEST)
    activated = jnp.maximum(aggregate + out_bias[None, None, :], 0.0).astype(jnp.bfloat16)
    return activated.reshape(vertex_rows, column_count)

LANES = 128
GROUPS = 4
PLANE = 4
PIECES = 2
MESH = pl.DeviceIdType.MESH


def picked_rows(index, table_ref, groups):
    depth = table_ref.shape[0]
    group = index // depth
    within = index - group * depth
    positions = lax.broadcasted_iota(jnp.int32, (index.shape[0], depth), 1)
    chosen = (positions == within).astype(jnp.float32).astype(jnp.bfloat16)
    every = jnp.dot(chosen, table_ref[...], preferred_element_type=jnp.float32)
    width = table_ref.shape[1] // groups
    result = every[:, :width]
    for number in range(1, groups):
        part = every[:, number * width : (number + 1) * width]
        result = jnp.where(group == number, part, result)
    return result.astype(jnp.bfloat16)


def over_rows(left, right):
    dims = (((0,), (0,)), ((), ()))
    return lax.dot_general(left, right, dims, preferred_element_type=jnp.float32)


def exchange_kernel(
    count, features_hbm, weight_hbm, send_hbm, hub_ref, extended_ref,
    features_ref, weight_ref, send_ref, load_sems,
    other_ref, total_ref, table_ref, index_ref, packed_ref, own_hubs_ref, hubs_ref,
    feature_sems, send_sems, receive_sems, hub_send_sems, hub_receive_sems,
):
    part = lax.axis_index("dom")
    feat = lax.axis_index("feat")
    depth, vertex_rows = features_ref.shape
    width = extended_ref.shape[1]
    loads = []
    for number, (source, target) in enumerate(
        ((weight_hbm, weight_ref), (features_hbm, features_ref), (send_hbm, send_ref))
    ):
        loads.append(pltpu.make_async_copy(source, target, load_sems.at[number]))
        loads[number].start()
    lines = count // PLANE
    line = part // PLANE
    group_rows = vertex_rows // GROUPS
    slots, half_rows = send_ref.shape
    chunk = half_rows // PIECES
    offsets = list(range(-REACH, 0)) + list(range(1, REACH + 1))
    hub_total = hub_ref.shape[1]
    halo_end = vertex_rows + slots * half_rows

    barrier = pltpu.get_barrier_semaphore()
    pl.semaphore_signal(barrier, inc=1, device_id=(part, 1 - feat), device_id_type=MESH)

    def greet(step, carry):
        peer = lax.rem(part + step * PLANE, count)
        pl.semaphore_signal(barrier, inc=1, device_id=(peer, feat), device_id_type=MESH)
        return carry

    lax.fori_loop(1, lines, greet, 0)
    greeted = lines
    for offset in offsets:
        if abs(offset) % PLANE != 0:
            target = part + offset
            inside = (target >= 0) & (target < count)
            greeted = greeted + inside.astype(jnp.int32)

            @pl.when(inside)
            def _():
                pl.semaphore_signal(
                    barrier, inc=1, device_id=(target, feat), device_id_type=MESH
                )

    hub_row = hub_ref[...]
    hub_col = jnp.transpose(jnp.broadcast_to(hub_row, (8, hub_total)))[:, :1]
    owner_row = hub_row // vertex_rows
    owner_col = hub_col // vertex_rows
    same = owner_row == owner_col
    first = lax.broadcasted_iota(jnp.int32, (hub_total, hub_total), 0)
    second = lax.broadcasted_iota(jnp.int32, (hub_total, hub_total), 1)
    rank_row = jnp.sum(jnp.where(same & (first < second), 1.0, 0.0), 0, keepdims=True)
    rank_col = jnp.sum(jnp.where(same & (second < first), 1.0, 0.0), 1, keepdims=True)
    rank_row = rank_row.astype(jnp.int32)
    rank_col = rank_col.astype(jnp.int32)
    ranks = lax.broadcasted_iota(jnp.int32, (HUB_MOST, hub_total), 0)
    chosen = (rank_row == ranks) & (owner_row == part)
    local_row = (hub_row - part * vertex_rows).astype(jnp.float32)
    own_index = jnp.sum(jnp.where(chosen, local_row, 0.0), 1, keepdims=True).astype(jnp.int32)
    loads[0].wait()
    loads[1].wait()
    columns = pl.ds(pl.multiple_of(feat * width, width), width)
    own_weight = weight_ref[pl.ds(pl.multiple_of(feat * depth, 16), depth), columns]
    other_weight = weight_ref[pl.ds(pl.multiple_of((1 - feat) * depth, 16), depth), columns]
    total_ref[...] = over_rows(own_weight, features_ref[...])
    loads[2].wait()
    index_ref[...] = jnp.transpose(send_ref[...])

    pl.semaphore_wait(barrier, greeted)

    exchanges = []
    for group in range(GROUPS):
        columns = pl.ds(group * group_rows, group_rows)
        exchanges.append(
            pltpu.make_async_remote_copy(
                src_ref=features_hbm.at[:, columns], dst_ref=other_ref.at[:, columns],
                send_sem=feature_sems.at[0, group], recv_sem=feature_sems.at[1, group],
                device_id=(part, 1 - feat), device_id_type=MESH,
            )
        )
        exchanges[group].start()
    for group in range(GROUPS):
        rows = pl.ds(group * group_rows, group_rows)
        exchanges[group].wait_recv()
        projected = total_ref[:, rows] + over_rows(other_weight, other_ref[:, rows])
        projected = jnp.transpose(projected).astype(jnp.bfloat16)
        extended_ref[rows, :] = projected
        table_ref[:, group * width : (group + 1) * width] = projected

    own_hubs = picked_rows(own_index, table_ref, GROUPS)
    own_hubs_ref[...] = own_hubs
    hubs_ref[pl.ds(pl.multiple_of(part * HUB_MOST, 16), HUB_MOST), :] = own_hubs

    def hub_copy(number, first, blocks, target, source_ref=None):
        rows = pl.ds(pl.multiple_of(first * HUB_MOST, 16), blocks * HUB_MOST)
        return pltpu.make_async_remote_copy(
            src_ref=hubs_ref.at[rows, :] if source_ref is None else source_ref,
            dst_ref=hubs_ref.at[rows, :],
            send_sem=hub_send_sems.at[number], recv_sem=hub_receive_sems.at[number],
            device_id=(target, feat), device_id_type=MESH,
        )

    side = lax.rem(part, 2)
    across = part + 1 - 2 * side
    pair = part - side
    pair_side = lax.rem(part // 2, 2)
    far = part + 2 - 4 * pair_side
    far_pair = pair + 2 - 4 * pair_side
    plane = line * PLANE

    def line_copy(step, first):
        return hub_copy(1 + step, first, PLANE, lax.rem(part + step * PLANE, count))

    hub_copy(0, part, 1, across, own_hubs_ref).start()

    def halo_copy(slot, piece):
        rows = pl.ds(vertex_rows + slot * half_rows + piece * chunk, chunk)
        return pltpu.make_async_remote_copy(
            src_ref=packed_ref.at[slot, piece * chunk : (piece + 1) * chunk, :], dst_ref=extended_ref.at[rows, :],
            send_sem=send_sems.at[slot, piece], recv_sem=receive_sems.at[slot, piece],
            device_id=(lax.rem(part + offsets[slot] + count, count), feat), device_id_type=MESH,
        )

    order = sorted(range(slots), key=lambda slot: (abs(offsets[slot]) % 2 == 0, -abs(offsets[slot])))
    for number, slot in enumerate(order):
        if number == 2:
            hub_copy(0, across, 1, across, own_hubs_ref).wait_recv()
            hub_copy(1, pair, 2, far).start()
        if number == 5:
            hub_copy(1, far_pair, 2, far).wait_recv()
            for step in range(1, lines):
                line_copy(step, plane).start()
        target = part + offsets[slot]
        present = (target >= 0) & (target < count)

        @pl.when(present)
        def _():
            for piece in range(PIECES):
                rows = pl.ds(piece * chunk, chunk)
                index = index_ref[rows, slot : slot + 1]
                packed_ref[slot, rows, :] = picked_rows(index, table_ref, GROUPS)
                halo_copy(slot, piece).start()

        source = part - offsets[slot]

        @pl.when((source < 0) | (source >= count))
        def _():
            rows = pl.ds(vertex_rows + slot * half_rows, half_rows)
            extended_ref[rows, :] = jnp.zeros((half_rows, width), jnp.bfloat16)

    for step in range(1, lines):
        line_copy(step, lax.rem(line - step + lines, lines) * PLANE).wait_recv()
    place = owner_col * HUB_MOST + rank_col
    extended_ref[halo_end : halo_end + hub_total, :] = picked_rows(place, hubs_ref, 1)
    for exchange in exchanges:
        exchange.wait_send()
    hub_copy(0, part, 1, across, own_hubs_ref).wait_send()
    hub_copy(1, pair, 2, far).wait_send()
    for step in range(1, lines):
        line_copy(step, plane).wait_send()
    for slot in order:
        source = part - offsets[slot]
        target = part + offsets[slot]

        @pl.when((source >= 0) & (source < count))
        def _():
            for piece in range(PIECES):
                halo_copy(slot, piece).wait_recv()

        @pl.when((target >= 0) & (target < count))
        def _():
            for piece in range(PIECES):
                halo_copy(slot, piece).wait_send()


def tiles_kernel(
    rows_ref, cols_ref, count_ref, values_ref, extended_ref, bias_ref, out_ref, total_ref
):
    slots, edge, _ = values_ref.shape
    width = out_ref.shape[1]
    spare = out_ref.shape[0] // edge
    live = count_ref[0]
    total_ref[...] = jnp.zeros_like(total_ref)
    together = math.gcd(slots, 12)

    def step(number, carry):
        products, places = [], []
        for inner in range(together):
            slot = number * together + inner
            block = pl.ds(pl.multiple_of(cols_ref[slot] * edge, edge), edge)
            places.append(jnp.where(slot < live, rows_ref[slot], spare))
            products.append(
                jnp.dot(values_ref[slot], extended_ref[block, :], preferred_element_type=jnp.float32)
            )
        for place, product in zip(places, products):
            total_ref[pl.ds(pl.multiple_of(place * edge, edge), edge), :] += product
        return carry

    lax.fori_loop(0, (live + together - 1) // together, step, 0)
    summed = total_ref[: out_ref.shape[0], :] + bias_ref[...]
    out_ref[...] = jnp.maximum(summed, 0.0).astype(jnp.bfloat16)


def local(
    features, weight, out_bias, tile_values, tile_rows, tile_cols, tile_count, send_rows, hub_ids
):
    width = out_bias.shape[0]
    vertex_rows, depth = features.shape
    count = lax.axis_size("dom")
    _, slots, half_rows = send_rows.shape
    hub_total = hub_ids.shape[0]
    edge = tile_values.shape[1]
    vmem = pl.BlockSpec(memory_space=pltpu.VMEM)
    smem = pl.BlockSpec(memory_space=pltpu.SMEM)
    extended_rows = vertex_rows + slots * half_rows + hub_total
    extended = pl.pallas_call(
        functools.partial(exchange_kernel, count),
        out_shape=jax.ShapeDtypeStruct((extended_rows, width), jnp.bfloat16),
        in_specs=[pl.BlockSpec(memory_space=pltpu.HBM)] * 3 + [vmem],
        out_specs=vmem,
        scratch_shapes=[
            pltpu.VMEM((depth, vertex_rows), jnp.bfloat16),
            pltpu.VMEM(weight.shape, jnp.bfloat16),
            pltpu.VMEM((slots, half_rows), jnp.int32),
            pltpu.SemaphoreType.DMA((3,)),
            pltpu.VMEM((depth, vertex_rows), jnp.bfloat16),
            pltpu.VMEM((width, vertex_rows), jnp.float32),
            pltpu.VMEM((vertex_rows // GROUPS, GROUPS * width), jnp.bfloat16),
            pltpu.VMEM((half_rows, slots), jnp.int32),
            pltpu.VMEM((slots, half_rows, width), jnp.bfloat16),
            pltpu.VMEM((HUB_MOST, width), jnp.bfloat16),
            pltpu.VMEM((count * HUB_MOST, width), jnp.bfloat16),
            pltpu.SemaphoreType.DMA((2, GROUPS)),
            pltpu.SemaphoreType.DMA((slots, PIECES)),
            pltpu.SemaphoreType.DMA((slots, PIECES)),
            pltpu.SemaphoreType.DMA((count // PLANE + 1,)),
            pltpu.SemaphoreType.DMA((count // PLANE + 1,)),
        ],
        compiler_params=pltpu.CompilerParams(
            collective_id=0, has_side_effects=True, vmem_limit_bytes=32 << 20
        ),
    )(jnp.transpose(features), weight, send_rows[0], hub_ids[None, :])
    return pl.pallas_call(
        tiles_kernel,
        out_shape=jax.ShapeDtypeStruct((vertex_rows, width), jnp.bfloat16),
        in_specs=[smem] * 3 + [vmem] * 3,
        out_specs=vmem,
        scratch_shapes=[pltpu.VMEM((vertex_rows + edge, width), jnp.float32)],
        compiler_params=pltpu.CompilerParams(vmem_limit_bytes=24 << 20),
    )(tile_rows, tile_cols, tile_count, tile_values, extended, out_bias[None, :])


def solution(mesh):
    in_specs = (
        P("dom", "feat"),
        P(),
        P("feat"),
        P("dom", None, None),
        P("dom"),
        P("dom"),
        P("dom"),
        P("dom", None, None),
        P(),
    )
    out_specs = P("dom", "feat")

    def program(features, weight, out_bias, *rest):
        whole_lanes = out_bias.shape[0] % (LANES * mesh.shape["feat"]) == 0
        fits = mesh.shape["feat"] == 2 and mesh.shape["dom"] % PLANE == 0
        body = local if fits and whole_lanes else local_any
        return jax.shard_map(
            body, mesh=mesh, in_specs=in_specs, out_specs=out_specs, check_vma=False
        )(features, weight, out_bias, *rest)

    return program
```

profile of v0, /device:TPU:0, one launch (start us, length us, event | category | flops | bytes accessed | tf_op | source)
XLA Modules:
  0.0 47.0 jit_solution(8438306379774273769)
XLA Ops:
  0.0 0.0 copy-start
  0.8 0.0 copy-start.1
  0.8 1.4 %copy-done.1 = bf16[2048,304]{0,1:T(8,128)(2,1)S(1)} copy-done((bf16[2048,304]{0,1:T(8,128)(2,1)S(1)}, bf16[2048,304]{0,1:T(8,128)(2,1)}, u32[]{:S(2)}) %copy-start.1) | copy-done | bytes 1245208
  2.3 0.0 copy-start.2
  2.3 1.0 %copy-done.2 = bf16[608,256]{1,0:T(8,128)(2,1)S(1)} copy-done((bf16[608,256]{1,0:T(8,128)(2,1)S(1)}, bf16[608,256]{1,0:T(8,128)(2,1)}, u32[]{:S(2)}) %copy-start.2) | copy-done | bytes 311320
  3.2 0.0 copy-start.3
  3.2 0.8 %copy-done.3 = s32[1,8,1024]{2,1,0:T(8,128)S(1)} copy-done((s32[1,8,1024]{2,1,0:T(8,128)S(1)}, s32[1,8,1024]{2,1,0:T(8,128)}, u32[]{:S(2)}) %copy-start.3) | copy-done | bytes 32792
  4.0 0.0 copy-start.4
  4.0 0.7 %copy-done.4 = s32[256]{0:T(256)S(1)} copy-done((s32[256]{0:T(256)S(1)}, s32[256]{0:T(256)}, u32[]{:S(2)}) %copy-start.4) | copy-done | bytes 1048
  4.7 0.0 copy-start.5
  4.7 0.0 copy-start.6
  4.7 0.0 copy-start.7
  4.7 38.3 %shard_map.91.extended_ref = bf16[10496,128]{1,0:T(8,128)(2,1)S(1)} custom-call(bf16[304,2048]{1,0:T(8,128)(2,1)S(1)} %bitcast.4, bf16[608,256]{1,0:T(8,128)(2,1)S(1)} %copy-done.2, s32[8,1024]{1,0:T(8,128)S(1)} %bitcast.5, s32[1,256]{1,0:T(1,128)S(1)} %bitcast.6), custom_call_target="tpu_custom_call" | custom-call | tf_op jit(solution)/shard_map/pallas_call | solution.py:322
  43.0 0.0 copy-done
  43.0 0.0 copy-done.5
  43.0 0.0 copy-done.6
  43.0 0.0 copy-done.7
  43.0 4.0 %shard_map.92 = bf16[2048,128]{1,0:T(8,128)(2,1)} custom-call(s32[108]{0:T(128)S(1)} %copy-done.5, s32[108]{0:T(128)S(1)} %copy-done.6, s32[1]{0:T(128)S(6)} %copy.10.count_ref, bf16[108,128,128]{2,1,0:T(8,128)(2,1)S(1)} %copy-done, bf16[10496,128]{1,0:T(8,128)(2,1)S(1)} %shard_map.91.extended_ref, f32[1,128]{1,0:T(1,128)S(1)} %bitcast.7), custom_call_target="tpu_custom_call" | custom-call | tf_op jit(solution)/shard_map/pallas_call | solution.py:349
Async XLA Ops:
  0.0 43.0 %copy-start = (bf16[108,128,128]{2,1,0:T(8,128)(2,1)S(1)}, bf16[108,128,128]{2,1,0:T(8,128)(2,1)}, u32[]{:S(2)}) copy-start(bf16[108,128,128]{2,1,0:T(8,128)(2,1)} %values_ref.1) | copy-start | bytes 10616836
  0.8 1.5 %copy-start.1 = (bf16[2048,304]{0,1:T(8,128)(2,1)S(1)}, bf16[2048,304]{0,1:T(8,128)(2,1)}, u32[]{:S(2)}) copy-start(bf16[2048,304]{0,1:T(8,128)(2,1)} %param.9) | copy-start | bytes 3735556
  2.3 1.0 %copy-start.2 = (bf16[608,256]{1,0:T(8,128)(2,1)S(1)}, bf16[608,256]{1,0:T(8,128)(2,1)}, u32[]{:S(2)}) copy-start(bf16[608,256]{1,0:T(8,128)(2,1)} %weight_hbm.1) | copy-start | bytes 933892
  3.2 0.8 %copy-start.3 = (s32[1,8,1024]{2,1,0:T(8,128)S(1)}, s32[1,8,1024]{2,1,0:T(8,128)}, u32[]{:S(2)}) copy-start(s32[1,8,1024]{2,1,0:T(8,128)} %param.16) | copy-start | bytes 98308
  4.0 0.7 %copy-start.4 = (s32[256]{0:T(256)S(1)}, s32[256]{0:T(256)}, u32[]{:S(2)}) copy-start(s32[256]{0:T(256)} %param.17) | copy-start | bytes 3076
  4.7 38.3 %copy-start.5 = (s32[108]{0:T(128)S(1)}, s32[108]{0:T(128)}, u32[]{:S(2)}) copy-start(s32[108]{0:T(128)} %rows_ref.1) | copy-start | bytes 1300
  4.7 38.4 %copy-start.6 = (s32[108]{0:T(128)S(1)}, s32[108]{0:T(128)}, u32[]{:S(2)}) copy-start(s32[108]{0:T(128)} %cols_ref.1) | copy-start | bytes 1300
  4.7 38.4 %copy-start.7 = (f32[128]{0:T(128)S(1)}, f32[128]{0:T(128)}, u32[]{:S(2)}) copy-start(f32[128]{0:T(128)} %param.11) | copy-start | bytes 1540
where the time goes:
time: 46.9 us; the launch traced here: 47 us
  Pallas kernels  42.3 us (90%)
  local copies, waits for them, and re-layouts  3.87 us (8%)
  between operations  0.86 us (2%)
    pallas_call x1, Pallas kernels, local(): pl.pallas_call(functools.partial(exchange_kernel, count), out_shape=jax.S...  38.3 us
    pallas_call x1, Pallas kernels, local(): pl.pallas_call(tiles_kernel, out_shape=jax.ShapeDtypeStruct((vertex_rows,...  4 us
    unnamed x16, local copies, waits for them, and re-layouts  3.87 us

commit v1 on v0

--- a/solution.py
+++ b/solution.py
@@ -78,6 +78,9 @@
 GROUPS = 4
 PLANE = 4
 PIECES = 2
+HELD = 1
+OUTER_ORDER = (-1, 4, -3, 3, -2, 1, 2, -4)
+INNER_ORDER = (-3, 4, 1, -2, 3, -4, 2, -1)
 MESH = pl.DeviceIdType.MESH
 
 
@@ -102,9 +105,10 @@
 
 
 def exchange_kernel(
-    count, features_hbm, weight_hbm, send_hbm, hub_ref, extended_ref,
-    features_ref, weight_ref, send_ref, load_sems,
-    other_ref, total_ref, table_ref, index_ref, packed_ref, own_hubs_ref, hubs_ref,
+    count, features_hbm, weight_hbm, send_hbm, hub_hbm, extended_ref,
+    features_ref, weight_ref, send_ref, hub_ref, load_sems,
+    partial_ref, other_ref, total_ref, table_ref, ordered_ref, index_ref, packed_ref,
+    own_hubs_ref, hubs_ref, near_hubs_ref, far_hubs_ref,
     feature_sems, send_sems, receive_sems, hub_send_sems, hub_receive_sems,
 ):
     part = lax.axis_index("dom")
@@ -113,12 +117,16 @@
     width = extended_ref.shape[1]
     loads = []
     for number, (source, target) in enumerate(
-        ((weight_hbm, weight_ref), (features_hbm, features_ref), (send_hbm, send_ref))
+        (
+            (features_hbm, features_ref), (weight_hbm, weight_ref),
+            (hub_hbm, hub_ref), (send_hbm, send_ref),
+        )
     ):
         loads.append(pltpu.make_async_copy(source, target, load_sems.at[number]))
         loads[number].start()
     lines = count // PLANE
     line = part // PLANE
+    place = part - line * PLANE
     group_rows = vertex_rows // GROUPS
     slots, half_rows = send_ref.shape
     chunk = half_rows // PIECES
@@ -148,6 +156,35 @@
                     barrier, inc=1, device_id=(target, feat), device_id_type=MESH
                 )
 
+    outer = (place == 0) | (place == PLANE - 1)
+    sign = jnp.where(place < PLANE // 2, 1, -1)
+    ordered = [sign * jnp.where(outer, *pair) for pair in zip(OUTER_ORDER, INNER_ORDER)]
+    ordered_slots = [
+        jnp.where(offset < 0, offset + REACH, offset + REACH - 1) for offset in ordered
+    ]
+
+    loads[0].wait()
+    loads[1].wait()
+    own_depth = pl.ds(pl.multiple_of(feat * depth, 16), depth)
+    own_columns = pl.ds(pl.multiple_of(feat * width, width), width)
+    other_columns = pl.ds(pl.multiple_of((1 - feat) * width, width), width)
+    partial_ref[...] = over_rows(weight_ref[own_depth, other_columns], features_ref[...])
+
+    pl.semaphore_wait(barrier, greeted)
+
+    exchanges = []
+    for group in range(GROUPS):
+        columns = pl.ds(group * group_rows, group_rows)
+        exchanges.append(
+            pltpu.make_async_remote_copy(
+                src_ref=partial_ref.at[:, columns], dst_ref=other_ref.at[:, columns],
+                send_sem=feature_sems.at[0, group], recv_sem=feature_sems.at[1, group],
+                device_id=(part, 1 - feat), device_id_type=MESH,
+            )
+        )
+        exchanges[group].start()
+    total_ref[...] = over_rows(weight_ref[own_depth, own_columns], features_ref[...])
+    loads[2].wait()
     hub_row = hub_ref[...]
     hub_col = jnp.transpose(jnp.broadcast_to(hub_row, (8, hub_total)))[:, :1]
     owner_row = hub_row // vertex_rows
@@ -163,39 +200,22 @@
     chosen = (rank_row == ranks) & (owner_row == part)
     local_row = (hub_row - part * vertex_rows).astype(jnp.float32)
     own_index = jnp.sum(jnp.where(chosen, local_row, 0.0), 1, keepdims=True).astype(jnp.int32)
-    loads[0].wait()
-    loads[1].wait()
-    columns = pl.ds(pl.multiple_of(feat * width, width), width)
-    own_weight = weight_ref[pl.ds(pl.multiple_of(feat * depth, 16), depth), columns]
-    other_weight = weight_ref[pl.ds(pl.multiple_of((1 - feat) * depth, 16), depth), columns]
-    total_ref[...] = over_rows(own_weight, features_ref[...])
-    loads[2].wait()
-    index_ref[...] = jnp.transpose(send_ref[...])
-
-    pl.semaphore_wait(barrier, greeted)
-
-    exchanges = []
-    for group in range(GROUPS):
-        columns = pl.ds(group * group_rows, group_rows)
-        exchanges.append(
-            pltpu.make_async_remote_copy(
-                src_ref=features_hbm.at[:, columns], dst_ref=other_ref.at[:, columns],
-                send_sem=feature_sems.at[0, group], recv_sem=feature_sems.at[1, group],
-                device_id=(part, 1 - feat), device_id_type=MESH,
-            )
-        )
-        exchanges[group].start()
+    loads[3].wait()
+    for number, slot in enumerate(ordered_slots):
+        ordered_ref[number : number + 1, :] = send_ref[pl.ds(slot, 1), :]
+    index_ref[...] = jnp.transpose(ordered_ref[...])
+
     for group in range(GROUPS):
         rows = pl.ds(group * group_rows, group_rows)
         exchanges[group].wait_recv()
-        projected = total_ref[:, rows] + over_rows(other_weight, other_ref[:, rows])
-        projected = jnp.transpose(projected).astype(jnp.bfloat16)
+        projected = jnp.transpose(total_ref[:, rows] + other_ref[:, rows]).astype(jnp.bfloat16)
         extended_ref[rows, :] = projected
         table_ref[:, group * width : (group + 1) * width] = projected
 
     own_hubs = picked_rows(own_index, table_ref, GROUPS)
     own_hubs_ref[...] = own_hubs
-    hubs_ref[pl.ds(pl.multiple_of(part * HUB_MOST, 16), HUB_MOST), :] = own_hubs
+    hub_home = (place * lines + line) * HUB_MOST
+    hubs_ref[pl.ds(pl.multiple_of(hub_home, 16), HUB_MOST), :] = own_hubs
 
     def hub_copy(number, first, blocks, target, source_ref=None):
         rows = pl.ds(pl.multiple_of(first * HUB_MOST, 16), blocks * HUB_MOST)
@@ -206,87 +226,153 @@
             device_id=(target, feat), device_id_type=MESH,
         )
 
-    side = lax.rem(part, 2)
+    side = lax.rem(place, 2)
     across = part + 1 - 2 * side
-    pair = part - side
-    pair_side = lax.rem(part // 2, 2)
+    across_place = place + 1 - 2 * side
+    pair_place = place - side
+    pair_side = place // 2
     far = part + 2 - 4 * pair_side
-    far_pair = pair + 2 - 4 * pair_side
-    plane = line * PLANE
-
-    def line_copy(step, first):
-        return hub_copy(1 + step, first, PLANE, lax.rem(part + step * PLANE, count))
-
-    hub_copy(0, part, 1, across, own_hubs_ref).start()
-
-    def halo_copy(slot, piece):
-        rows = pl.ds(vertex_rows + slot * half_rows + piece * chunk, chunk)
+
+    def line_copy(step, from_line):
+        target = lax.rem(part + step * PLANE, count)
+        return hub_copy(1 + step, place * lines + from_line, 1, target, own_hubs_ref)
+
+    for step in range(1, lines):
+        line_copy(step, line).start()
+
+    def halo_copy(number, slot, offset, piece):
+        start = vertex_rows + slot * half_rows + piece * chunk
+        rows = pl.ds(pl.multiple_of(start, 16), chunk)
         return pltpu.make_async_remote_copy(
-            src_ref=packed_ref.at[slot, piece * chunk : (piece + 1) * chunk, :], dst_ref=extended_ref.at[rows, :],
-            send_sem=send_sems.at[slot, piece], recv_sem=receive_sems.at[slot, piece],
-            device_id=(lax.rem(part + offsets[slot] + count, count), feat), device_id_type=MESH,
+            src_ref=packed_ref.at[number, piece * chunk : (piece + 1) * chunk, :],
+            dst_ref=extended_ref.at[rows, :],
+            send_sem=send_sems.at[number, piece], recv_sem=receive_sems.at[slot, piece],
+            device_id=(lax.rem(part + offset + count, count), feat), device_id_type=MESH,
         )
 
-    order = sorted(range(slots), key=lambda slot: (abs(offsets[slot]) % 2 == 0, -abs(offsets[slot])))
-    for number, slot in enumerate(order):
-        if number == 2:
-            hub_copy(0, across, 1, across, own_hubs_ref).wait_recv()
-            hub_copy(1, pair, 2, far).start()
-        if number == 5:
-            hub_copy(1, far_pair, 2, far).wait_recv()
-            for step in range(1, lines):
-                line_copy(step, plane).start()
-        target = part + offsets[slot]
-        present = (target >= 0) & (target < count)
-
-        @pl.when(present)
+    def present(number):
+        target = part + ordered[number]
+        return (target >= 0) & (target < count)
+
+    def wait_sent(number, pieces):
+        for piece in pieces:
+            halo_copy(number, ordered_slots[number], ordered[number], piece).wait_send()
+
+    early = range(PIECES - HELD)
+    late = range(PIECES - HELD, PIECES)
+
+    def gate(number, also=True):
+        @pl.when(present(number) & also)
+        def _():
+            wait_sent(number, early)
+
+    def pick(number):
+        @pl.when(present(number))
         def _():
             for piece in range(PIECES):
                 rows = pl.ds(piece * chunk, chunk)
-                index = index_ref[rows, slot : slot + 1]
-                packed_ref[slot, rows, :] = picked_rows(index, table_ref, GROUPS)
-                halo_copy(slot, piece).start()
-
-        source = part - offsets[slot]
+                index = index_ref[rows, number : number + 1]
+                packed_ref[number, rows, :] = picked_rows(index, table_ref, GROUPS)
+                if number < 2:
+                    halo_copy(number, ordered_slots[number], ordered[number], piece).start()
+
+    def send(number, also=True):
+        @pl.when(present(number) & also)
+        def _():
+            for piece in range(PIECES):
+                halo_copy(number, ordered_slots[number], ordered[number], piece).start()
+
+    inner = jnp.logical_not(outer)
+    pick(0)
+    pick(1)
+    pick(2)
+    for step in range(1, lines):
+        line_copy(step, lax.rem(line - step + lines, lines)).wait_recv()
+    hub_copy(0, place * lines, lines, across).start()
+    pick(3)
+    gate(0)
+    send(2)
+    send(3, inner)
+    pick(4)
+    pick(5)
+    pick(6)
+    pick(7)
+    gate(2)
+    send(3, outer)
+    send(4)
+    send(5)
+    hub_copy(0, across_place * lines, lines, across).wait_recv()
+    pair_rows = 2 * lines * HUB_MOST
+    pair_start = pair_place * lines * HUB_MOST
+    owner_line = owner_col // PLANE
+    owner_place = owner_col - owner_line * PLANE
+    within = (owner_place * lines + owner_line) * HUB_MOST + rank_col - pair_start
+    positions = lax.broadcasted_iota(jnp.int32, (hub_total, pair_rows), 1)
+    chosen = (positions == within).astype(jnp.float32).astype(jnp.bfloat16)
+    pair_hubs = hubs_ref[pl.ds(pl.multiple_of(pair_start, 16), pair_rows), :]
+    near_hubs = jnp.dot(chosen, pair_hubs, preferred_element_type=jnp.float32)
+    near_hubs_ref[...] = near_hubs.astype(jnp.bfloat16)
+    hub_exchange = pltpu.make_async_remote_copy(
+        src_ref=near_hubs_ref, dst_ref=far_hubs_ref,
+        send_sem=hub_send_sems.at[1], recv_sem=hub_receive_sems.at[1],
+        device_id=(far, feat), device_id_type=MESH,
+    )
+    hub_exchange.start()
+    gate(3)
+    gate(4)
+    send(6)
+    send(7)
+
+    for slot, offset in enumerate(offsets):
+        source = part - offset
 
         @pl.when((source < 0) | (source >= count))
         def _():
             rows = pl.ds(vertex_rows + slot * half_rows, half_rows)
             extended_ref[rows, :] = jnp.zeros((half_rows, width), jnp.bfloat16)
 
-    for step in range(1, lines):
-        line_copy(step, lax.rem(line - step + lines, lines) * PLANE).wait_recv()
-    place = owner_col * HUB_MOST + rank_col
-    extended_ref[halo_end : halo_end + hub_total, :] = picked_rows(place, hubs_ref, 1)
+    hub_exchange.wait_recv()
+    hubs = near_hubs_ref[...].astype(jnp.float32) + far_hubs_ref[...].astype(jnp.float32)
+    extended_ref[halo_end : halo_end + hub_total, :] = hubs.astype(jnp.bfloat16)
     for exchange in exchanges:
         exchange.wait_send()
-    hub_copy(0, part, 1, across, own_hubs_ref).wait_send()
-    hub_copy(1, pair, 2, far).wait_send()
+    hub_copy(0, place * lines, lines, across).wait_send()
+    hub_exchange.wait_send()
     for step in range(1, lines):
-        line_copy(step, plane).wait_send()
-    for slot in order:
-        source = part - offsets[slot]
-        target = part + offsets[slot]
+        line_copy(step, line).wait_send()
+    for number in range(slots):
+        gated = number in (0, 2, 3, 4)
+
+        @pl.when(present(number))
+        def _():
+            wait_sent(number, late if gated else range(PIECES))
+
+    for slot, offset in enumerate(offsets):
+        source = part - offset
 
         @pl.when((source >= 0) & (source < count))
         def _():
             for piece in range(PIECES):
-                halo_copy(slot, piece).wait_recv()
-
-        @pl.when((target >= 0) & (target < count))
-        def _():
-            for piece in range(PIECES):
-                halo_copy(slot, piece).wait_send()
+                halo_copy(0, slot, offset, piece).wait_recv()
 
 
 def tiles_kernel(
-    rows_ref, cols_ref, count_ref, values_ref, extended_ref, bias_ref, out_ref, total_ref
+    rows_in, cols_in, count_ref, values_ref, extended_ref, bias_ref, out_ref,
+    total_ref, rows_ref, cols_ref, sems,
 ):
+    loads = []
+    for number, (source, target) in enumerate(
+        ((rows_in, rows_ref), (cols_in, cols_ref))
+    ):
+        loads.append(pltpu.make_async_copy(source, target, sems.at[number]))
+        loads[number].start()
     slots, edge, _ = values_ref.shape
     width = out_ref.shape[1]
     spare = out_ref.shape[0] // edge
+    total_ref[...] = jnp.zeros_like(total_ref)
+    for load in loads:
+        load.wait()
     live = count_ref[0]
-    total_ref[...] = jnp.zeros_like(total_ref)
     together = math.gcd(slots, 12)
 
     def step(number, carry):
@@ -317,25 +403,29 @@
     hub_total = hub_ids.shape[0]
     edge = tile_values.shape[1]
     vmem = pl.BlockSpec(memory_space=pltpu.VMEM)
-    smem = pl.BlockSpec(memory_space=pltpu.SMEM)
     extended_rows = vertex_rows + slots * half_rows + hub_total
     extended = pl.pallas_call(
         functools.partial(exchange_kernel, count),
         out_shape=jax.ShapeDtypeStruct((extended_rows, width), jnp.bfloat16),
-        in_specs=[pl.BlockSpec(memory_space=pltpu.HBM)] * 3 + [vmem],
+        in_specs=[pl.BlockSpec(memory_space=pltpu.HBM)] * 4,
         out_specs=vmem,
         scratch_shapes=[
             pltpu.VMEM((depth, vertex_rows), jnp.bfloat16),
             pltpu.VMEM(weight.shape, jnp.bfloat16),
             pltpu.VMEM((slots, half_rows), jnp.int32),
-            pltpu.SemaphoreType.DMA((3,)),
-            pltpu.VMEM((depth, vertex_rows), jnp.bfloat16),
+            pltpu.VMEM((1, hub_total), jnp.int32),
+            pltpu.SemaphoreType.DMA((4,)),
+            pltpu.VMEM((width, vertex_rows), jnp.float32),
+            pltpu.VMEM((width, vertex_rows), jnp.float32),
             pltpu.VMEM((width, vertex_rows), jnp.float32),
             pltpu.VMEM((vertex_rows // GROUPS, GROUPS * width), jnp.bfloat16),
+            pltpu.VMEM((slots, half_rows), jnp.int32),
             pltpu.VMEM((half_rows, slots), jnp.int32),
             pltpu.VMEM((slots, half_rows, width), jnp.bfloat16),
             pltpu.VMEM((HUB_MOST, width), jnp.bfloat16),
             pltpu.VMEM((count * HUB_MOST, width), jnp.bfloat16),
+            pltpu.VMEM((hub_total, width), jnp.bfloat16),
+            pltpu.VMEM((hub_total, width), jnp.bfloat16),
             pltpu.SemaphoreType.DMA((2, GROUPS)),
             pltpu.SemaphoreType.DMA((slots, PIECES)),
             pltpu.SemaphoreType.DMA((slots, PIECES)),
@@ -345,15 +435,32 @@
         compiler_params=pltpu.CompilerParams(
             collective_id=0, has_side_effects=True, vmem_limit_bytes=32 << 20
         ),
-    )(jnp.transpose(features), weight, send_rows[0], hub_ids[None, :])
+    )(
+        *[
+            pltpu.with_memory_space_constraint(value, pltpu.HBM)
+            for value in (jnp.transpose(features), weight, send_rows[0], hub_ids[None, :])
+        ]
+    )
     return pl.pallas_call(
         tiles_kernel,
         out_shape=jax.ShapeDtypeStruct((vertex_rows, width), jnp.bfloat16),
-        in_specs=[smem] * 3 + [vmem] * 3,
+        in_specs=[vmem] * 2 + [pl.BlockSpec(memory_space=pltpu.SMEM)] + [vmem] * 3,
         out_specs=vmem,
-        scratch_shapes=[pltpu.VMEM((vertex_rows + edge, width), jnp.float32)],
+        scratch_shapes=[
+            pltpu.VMEM((vertex_rows + edge, width), jnp.float32),
+            pltpu.SMEM(tile_rows.shape, jnp.int32),
+            pltpu.SMEM(tile_cols.shape, jnp.int32),
+            pltpu.SemaphoreType.DMA((2,)),
+        ],
         compiler_params=pltpu.CompilerParams(vmem_limit_bytes=24 << 20),
-    )(tile_rows, tile_cols, tile_count, tile_values, extended, out_bias[None, :])
+    )(
+        tile_rows,
+        tile_cols,
+        tile_count,
+        tile_values,
+        extended,
+        out_bias[None, :],
+    )
 
 
 def solution(mesh):

time: 46.9 us -> 40.1 us (0.86)
  the two profiles are of different devices: /device:TPU:0 before, /device:TPU:21 now
where the time goes in v1:
time: 40.1 us; the launch traced here: 39.4 us
  Pallas kernels  38.5 us (96%)
  between operations  0.85 us (2%)
    pallas_call x1, Pallas kernels, local(): pl.pallas_call(functools.partial(exchange_kernel, count), out_shape=jax.S...  34.8 us
    pallas_call x1, Pallas kernels, local(): pl.pallas_call(tiles_kernel, out_shape=jax.ShapeDtypeStruct((vertex_rows,...  3.69 us

profile of v1, /device:TPU:21, one launch (start us, length us, event | category | flops | bytes accessed | tf_op | source)
XLA Modules:
  0.0 39.4 jit_solution(6030790719938330515)
XLA Ops:
  0.0 0.0 copy-start.2
  0.0 0.0 copy-start.1
  0.0 0.0 copy-start
  0.0 0.0 copy-start.3
  0.8 34.8 %shard_map.91.extended_ref = bf16[10496,128]{1,0:T(8,128)(2,1)S(1)} custom-call(bf16[304,2048]{1,0:T(8,128)(2,1)} %bitcast.5, bf16[608,256]{1,0:T(8,128)(2,1)} %weight_hbm.1, s32[8,1024]{1,0:T(8,128)} %bitcast.6, s32[1,256]{1,0:T(1,128)} %bitcast.7), custom_call_target="tpu_custom_call" | custom-call | tf_op jit(solution)/shard_map/pallas_call | solution.py:407
  35.6 0.0 copy-done.2
  35.6 0.0 copy-done.1
  35.6 0.0 copy-done
  35.7 0.0 copy-done.3
  35.7 3.7 %shard_map.92 = bf16[2048,128]{1,0:T(8,128)(2,1)} custom-call(s32[108]{0:T(128)S(1)} %copy-done.1, s32[108]{0:T(128)S(1)} %copy-done.2, s32[1]{0:T(128)S(6)} %copy.10.count_ref, bf16[108,128,128]{2,1,0:T(8,128)(2,1)S(1)} %copy-done, bf16[10496,128]{1,0:T(8,128)(2,1)S(1)} %shard_map.91.extended_ref, f32[1,128]{1,0:T(1,128)S(1)} %bitcast.4), custom_call_target="tpu_custom_call" | custom-call | tf_op jit(solution)/shard_map/pallas_call | solution.py:444
Async XLA Ops:
  0.0 35.6 %copy-start.2 = (s32[108]{0:T(128)S(1)}, s32[108]{0:T(128)}, u32[]{:S(2)}) copy-start(s32[108]{0:T(128)} %cols_in.1) | copy-start | bytes 1300
  0.0 35.6 %copy-start.1 = (s32[108]{0:T(128)S(1)}, s32[108]{0:T(128)}, u32[]{:S(2)}) copy-start(s32[108]{0:T(128)} %rows_in.1) | copy-start | bytes 1300
  0.0 35.6 %copy-start = (bf16[108,128,128]{2,1,0:T(8,128)(2,1)S(1)}, bf16[108,128,128]{2,1,0:T(8,128)(2,1)}, u32[]{:S(2)}) copy-start(bf16[108,128,128]{2,1,0:T(8,128)(2,1)} %values_ref.1) | copy-start | bytes 10616836
  0.0 35.6 %copy-start.3 = (f32[128]{0:T(128)S(1)}, f32[128]{0:T(128)}, u32[]{:S(2)}) copy-start(f32[128]{0:T(128)} %param.11) | copy-start | bytes 1540

commit v2 on v1

--- a/solution.py
+++ b/solution.py
@@ -77,8 +77,9 @@
 LANES = 128
 GROUPS = 4
 PLANE = 4
-PIECES = 2
+PIECES = 4
 HELD = 1
+EARLY = 5
 OUTER_ORDER = (-1, 4, -3, 3, -2, 1, 2, -4)
 INNER_ORDER = (-3, 4, 1, -2, 3, -4, 2, -1)
 MESH = pl.DeviceIdType.MESH
@@ -104,9 +105,66 @@
     return lax.dot_general(left, right, dims, preferred_element_type=jnp.float32)
 
 
+def arrange_tiles(
+    live, rows, cols, own_blocks, slot_blocks, present_slots, early_slots, early_meta_ref, late_ref
+):
+    total = rows.shape[1]
+    square = (total, total)
+    down = lax.broadcasted_iota(jnp.int32, square, 0)
+    along = lax.broadcasted_iota(jnp.int32, square, 1)
+    lane = lax.broadcasted_iota(jnp.int32, rows.shape, 1)
+    early = (cols < own_blocks).astype(jnp.int32)
+    is_live = (lane < live).astype(jnp.int32)
+    for number, (present, flag) in enumerate(zip(present_slots, early_slots)):
+        start = own_blocks + number * slot_blocks
+        inside = ((cols >= start) & (cols < start + slot_blocks)).astype(jnp.int32)
+        early = early + inside * flag.astype(jnp.int32)
+        is_live = is_live * (1 - inside * (1 - present.astype(jnp.int32)))
+    early = early * is_live
+    late = is_live - early
+
+    def upright(row):
+        return jnp.transpose(jnp.broadcast_to(row, (8, total)))[:, :1]
+
+    def places_of(key, key_col):
+        before = (key_col < key) | ((key_col == key) & (down < along))
+        return upright(jnp.sum(before.astype(jnp.int32), 0, keepdims=True))
+
+    def moved(places, column, shift=0):
+        return jnp.sum(jnp.where(places + shift == along, column, 0), 0, keepdims=True)
+
+    rows_col, cols_col = upright(rows), upright(cols)
+    slot_col = down[:, :1]
+    last = jnp.int32(1 << 20)
+    early_key = jnp.where(early > 0, rows, last)
+    early_col = jnp.where(upright(early) > 0, rows_col, last)
+    places = places_of(early_key, early_col)
+    key_sorted = moved(places, early_col)
+    key_before = moved(places, early_col, 1)
+    same = (key_sorted == key_before) & (lane > 0)
+    counted = jnp.sum((early_col == along).astype(jnp.int32), 0, keepdims=True)
+    ended = jnp.sum((early_col <= along).astype(jnp.int32), 0, keepdims=True) - 1
+    early_meta_ref[0:1, :] = moved(places, slot_col)
+    early_meta_ref[1:2, :] = moved(places, cols_col)
+    early_meta_ref[2:3, :] = same.astype(jnp.int32)
+    early_meta_ref[3:4, :] = jnp.maximum(ended, 0)
+    early_meta_ref[4:5, :] = counted
+    early_meta_ref[5:8, :] = jnp.zeros((3, total), jnp.int32)
+    late_key = 1 - late
+    places = places_of(late_key, upright(late_key))
+    late_ref[0:1, :] = moved(places, slot_col)
+    late_ref[1:2, :] = moved(places, rows_col)
+    late_ref[2:3, :] = moved(places, cols_col)
+    late_spread = jnp.broadcast_to(upright(late), square)
+    late_ref[3:4, :] = jnp.sum(late_spread, 0, keepdims=True)
+    late_ref[4:8, :] = jnp.zeros((4, total), jnp.int32)
+
+
 def exchange_kernel(
-    count, features_hbm, weight_hbm, send_hbm, hub_hbm, extended_ref,
-    features_ref, weight_ref, send_ref, hub_ref, load_sems,
+    count, features_hbm, weight_hbm, send_hbm, hub_hbm, rows_hbm, cols_hbm, values_hbm, live_ref,
+    extended_ref, values_ref, early_total_ref, late_smem,
+    features_ref, weight_ref, send_ref, hub_ref, rows_ref, cols_ref, load_sems,
+    early_ref, early_meta_ref, late_ref, early_smem, sums_ref,
     partial_ref, other_ref, total_ref, table_ref, ordered_ref, index_ref, packed_ref,
     own_hubs_ref, hubs_ref, near_hubs_ref, far_hubs_ref,
     feature_sems, send_sems, receive_sems, hub_send_sems, hub_receive_sems,
@@ -114,25 +172,29 @@
     part = lax.axis_index("dom")
     feat = lax.axis_index("feat")
     depth, vertex_rows = features_ref.shape
-    width = extended_ref.shape[1]
+    width = extended_ref.shape[2]
     loads = []
+    group_rows = vertex_rows // GROUPS
+    feature_parts = [pl.ds(group * group_rows, group_rows) for group in range(GROUPS)]
     for number, (source, target) in enumerate(
-        (
-            (features_hbm, features_ref), (weight_hbm, weight_ref),
-            (hub_hbm, hub_ref), (send_hbm, send_ref),
-        )
+        [(weight_hbm, weight_ref)]
+        + [(features_hbm.at[:, rows], features_ref.at[:, rows]) for rows in feature_parts]
+        + [(hub_hbm, hub_ref), (send_hbm, send_ref), (rows_hbm, rows_ref), (cols_hbm, cols_ref)]
     ):
         loads.append(pltpu.make_async_copy(source, target, load_sems.at[number]))
         loads[number].start()
     lines = count // PLANE
     line = part // PLANE
     place = part - line * PLANE
-    group_rows = vertex_rows // GROUPS
     slots, half_rows = send_ref.shape
     chunk = half_rows // PIECES
     offsets = list(range(-REACH, 0)) + list(range(1, REACH + 1))
     hub_total = hub_ref.shape[1]
-    halo_end = vertex_rows + slots * half_rows
+    tile_slots, edge, _ = values_ref.shape
+    own_blocks = vertex_rows // edge
+    slot_blocks = half_rows // edge
+    piece_blocks = chunk // edge
+    hub_block = own_blocks + slots * slot_blocks
 
     barrier = pltpu.get_barrier_semaphore()
     pl.semaphore_signal(barrier, inc=1, device_id=(part, 1 - feat), device_id_type=MESH)
@@ -163,28 +225,44 @@
         jnp.where(offset < 0, offset + REACH, offset + REACH - 1) for offset in ordered
     ]
 
+    def arriving(offset):
+        source = part - offset
+        return (source >= 0) & (source < count)
+
+    def arrives_early(offset):
+        source_place = lax.rem(place - offset + 2 * PLANE, PLANE)
+        found = source_place < 0
+        for number, (order, turn) in enumerate(
+            ((OUTER_ORDER, 1), (INNER_ORDER, 1), (INNER_ORDER, -1), (OUTER_ORDER, -1))
+        ):
+            if turn * offset in order[:EARLY]:
+                found = found | (source_place == number)
+        return found & arriving(offset)
+
     loads[0].wait()
-    loads[1].wait()
     own_depth = pl.ds(pl.multiple_of(feat * depth, 16), depth)
     own_columns = pl.ds(pl.multiple_of(feat * width, width), width)
     other_columns = pl.ds(pl.multiple_of((1 - feat) * width, width), width)
-    partial_ref[...] = over_rows(weight_ref[own_depth, other_columns], features_ref[...])
-
-    pl.semaphore_wait(barrier, greeted)
-
     exchanges = []
-    for group in range(GROUPS):
-        columns = pl.ds(group * group_rows, group_rows)
+    for group, rows in enumerate(feature_parts):
+        loads[1 + group].wait()
+        partial_ref[:, rows] = over_rows(
+            weight_ref[own_depth, other_columns], features_ref[:, rows]
+        )
+        if group == 0:
+            pl.semaphore_wait(barrier, greeted)
         exchanges.append(
             pltpu.make_async_remote_copy(
-                src_ref=partial_ref.at[:, columns], dst_ref=other_ref.at[:, columns],
+                src_ref=partial_ref.at[:, rows], dst_ref=other_ref.at[:, rows],
                 send_sem=feature_sems.at[0, group], recv_sem=feature_sems.at[1, group],
                 device_id=(part, 1 - feat), device_id_type=MESH,
             )
         )
         exchanges[group].start()
+    values_load = pltpu.make_async_copy(values_hbm, values_ref, load_sems.at[5 + GROUPS])
+    values_load.start()
     total_ref[...] = over_rows(weight_ref[own_depth, own_columns], features_ref[...])
-    loads[2].wait()
+    loads[1 + GROUPS].wait()
     hub_row = hub_ref[...]
     hub_col = jnp.transpose(jnp.broadcast_to(hub_row, (8, hub_total)))[:, :1]
     owner_row = hub_row // vertex_rows
@@ -200,7 +278,7 @@
     chosen = (rank_row == ranks) & (owner_row == part)
     local_row = (hub_row - part * vertex_rows).astype(jnp.float32)
     own_index = jnp.sum(jnp.where(chosen, local_row, 0.0), 1, keepdims=True).astype(jnp.int32)
-    loads[3].wait()
+    loads[2 + GROUPS].wait()
     for number, slot in enumerate(ordered_slots):
         ordered_ref[number : number + 1, :] = send_ref[pl.ds(slot, 1), :]
     index_ref[...] = jnp.transpose(ordered_ref[...])
@@ -209,13 +287,11 @@
         rows = pl.ds(group * group_rows, group_rows)
         exchanges[group].wait_recv()
         projected = jnp.transpose(total_ref[:, rows] + other_ref[:, rows]).astype(jnp.bfloat16)
-        extended_ref[rows, :] = projected
+        group_blocks = group_rows // edge
+        early_ref[group * group_blocks : (group + 1) * group_blocks] = projected.reshape(
+            group_blocks, edge, width
+        )
         table_ref[:, group * width : (group + 1) * width] = projected
-
-    own_hubs = picked_rows(own_index, table_ref, GROUPS)
-    own_hubs_ref[...] = own_hubs
-    hub_home = (place * lines + line) * HUB_MOST
-    hubs_ref[pl.ds(pl.multiple_of(hub_home, 16), HUB_MOST), :] = own_hubs
 
     def hub_copy(number, first, blocks, target, source_ref=None):
         rows = pl.ds(pl.multiple_of(first * HUB_MOST, 16), blocks * HUB_MOST)
@@ -237,15 +313,13 @@
         target = lax.rem(part + step * PLANE, count)
         return hub_copy(1 + step, place * lines + from_line, 1, target, own_hubs_ref)
 
-    for step in range(1, lines):
-        line_copy(step, line).start()
-
     def halo_copy(number, slot, offset, piece):
-        start = vertex_rows + slot * half_rows + piece * chunk
-        rows = pl.ds(pl.multiple_of(start, 16), chunk)
+        landing_ref = early_ref if number < EARLY else extended_ref
+        start = own_blocks + slot * slot_blocks + piece * piece_blocks
+        blocks = pl.ds(start, piece_blocks)
         return pltpu.make_async_remote_copy(
-            src_ref=packed_ref.at[number, piece * chunk : (piece + 1) * chunk, :],
-            dst_ref=extended_ref.at[rows, :],
+            src_ref=packed_ref.at[number, pl.ds(piece * piece_blocks, piece_blocks)],
+            dst_ref=landing_ref.at[blocks],
             send_sem=send_sems.at[number, piece], recv_sem=receive_sems.at[slot, piece],
             device_id=(lax.rem(part + offset + count, count), feat), device_id_type=MESH,
         )
@@ -272,23 +346,28 @@
             for piece in range(PIECES):
                 rows = pl.ds(piece * chunk, chunk)
                 index = index_ref[rows, number : number + 1]
-                packed_ref[number, rows, :] = picked_rows(index, table_ref, GROUPS)
+                packed_ref[number, pl.ds(piece * piece_blocks, piece_blocks)] = picked_rows(
+                    index, table_ref, GROUPS
+                ).reshape(piece_blocks, edge, width)
                 if number < 2:
                     halo_copy(number, ordered_slots[number], ordered[number], piece).start()
 
-    def send(number, also=True):
+    def send(number, also=True, pieces=range(PIECES)):
         @pl.when(present(number) & also)
         def _():
-            for piece in range(PIECES):
+            for piece in pieces:
                 halo_copy(number, ordered_slots[number], ordered[number], piece).start()
 
     inner = jnp.logical_not(outer)
+    own_hubs = picked_rows(own_index, table_ref, GROUPS)
+    own_hubs_ref[...] = own_hubs
+    hub_home = (place * lines + line) * HUB_MOST
+    hubs_ref[pl.ds(pl.multiple_of(hub_home, 16), HUB_MOST), :] = own_hubs
+    for step in range(1, lines):
+        line_copy(step, line).start()
     pick(0)
     pick(1)
     pick(2)
-    for step in range(1, lines):
-        line_copy(step, lax.rem(line - step + lines, lines)).wait_recv()
-    hub_copy(0, place * lines, lines, across).start()
     pick(3)
     gate(0)
     send(2)
@@ -297,10 +376,28 @@
     pick(5)
     pick(6)
     pick(7)
+    for step in range(1, lines):
+        line_copy(step, lax.rem(line - step + lines, lines)).wait_recv()
+    loads[3 + GROUPS].wait()
+    loads[4 + GROUPS].wait()
+    arrange_tiles(
+        live_ref[0], rows_ref[...], cols_ref[...], own_blocks, slot_blocks,
+        [arriving(offset) for offset in offsets],
+        [arrives_early(offset) for offset in offsets], early_meta_ref, late_ref,
+    )
+    meta_copy = pltpu.make_async_copy(early_meta_ref, early_smem, load_sems.at[6 + GROUPS])
+    meta_copy.start()
+    late_copy = pltpu.make_async_copy(late_ref, late_smem, load_sems.at[7 + GROUPS])
+    late_copy.start()
     gate(2)
     send(3, outer)
     send(4)
+    hub_copy(0, place * lines, lines, across).start()
     send(5)
+    gate(3)
+    gate(4)
+    send(6, pieces=range(PIECES - 1))
+    send(7)
     hub_copy(0, across_place * lines, lines, across).wait_recv()
     pair_rows = 2 * lines * HUB_MOST
     pair_start = pair_place * lines * HUB_MOST
@@ -318,22 +415,41 @@
         device_id=(far, feat), device_id_type=MESH,
     )
     hub_exchange.start()
-    gate(3)
-    gate(4)
-    send(6)
-    send(7)
+    send(6, pieces=range(PIECES - 1, PIECES))
 
     for slot, offset in enumerate(offsets):
-        source = part - offset
-
-        @pl.when((source < 0) | (source >= count))
+
+        @pl.when(arrives_early(offset))
         def _():
-            rows = pl.ds(vertex_rows + slot * half_rows, half_rows)
-            extended_ref[rows, :] = jnp.zeros((half_rows, width), jnp.bfloat16)
+            for piece in range(PIECES):
+                halo_copy(0, slot, offset, piece).wait_recv()
+
+    values_load.wait()
+    meta_copy.wait()
+    late_copy.wait()
+    together = math.gcd(tile_slots, 12)
+
+    def step(number, running):
+        for inner in range(together):
+            entry = number * together + inner
+            product = jnp.dot(
+                values_ref[early_smem[0, entry]], early_ref[early_smem[1, entry]],
+                preferred_element_type=jnp.float32,
+            )
+            kept = jnp.broadcast_to(early_smem[2, entry], running.shape) > 0
+            running = jnp.where(kept, running, 0.0) + product
+            sums_ref[entry] = running
+        return running
+
+    lax.fori_loop(0, tile_slots // together, step, jnp.zeros((edge, width), jnp.float32))
+    for block in range(vertex_rows // edge):
+        summed = sums_ref[early_smem[3, block]]
+        kept = jnp.broadcast_to(early_smem[4, block], summed.shape) > 0
+        early_total_ref[block * edge : (block + 1) * edge, :] = jnp.where(kept, summed, 0.0)
 
     hub_exchange.wait_recv()
     hubs = near_hubs_ref[...].astype(jnp.float32) + far_hubs_ref[...].astype(jnp.float32)
-    extended_ref[halo_end : halo_end + hub_total, :] = hubs.astype(jnp.bfloat16)
+    extended_ref[hub_block:] = hubs.astype(jnp.bfloat16).reshape(hub_total // edge, edge, width)
     for exchange in exchanges:
         exchange.wait_send()
     hub_copy(0, place * lines, lines, across).wait_send()
@@ -348,41 +464,33 @@
             wait_sent(number, late if gated else range(PIECES))
 
     for slot, offset in enumerate(offsets):
-        source = part - offset
-
-        @pl.when((source >= 0) & (source < count))
+
+        @pl.when(arriving(offset) & jnp.logical_not(arrives_early(offset)))
         def _():
             for piece in range(PIECES):
-                halo_copy(0, slot, offset, piece).wait_recv()
+                halo_copy(EARLY, slot, offset, piece).wait_recv()
 
 
 def tiles_kernel(
-    rows_in, cols_in, count_ref, values_ref, extended_ref, bias_ref, out_ref,
-    total_ref, rows_ref, cols_ref, sems,
+    late_ref, values_ref, extended_ref, start_ref, bias_ref, out_ref, total_ref
 ):
-    loads = []
-    for number, (source, target) in enumerate(
-        ((rows_in, rows_ref), (cols_in, cols_ref))
-    ):
-        loads.append(pltpu.make_async_copy(source, target, sems.at[number]))
-        loads[number].start()
     slots, edge, _ = values_ref.shape
-    width = out_ref.shape[1]
     spare = out_ref.shape[0] // edge
-    total_ref[...] = jnp.zeros_like(total_ref)
-    for load in loads:
-        load.wait()
-    live = count_ref[0]
+    total_ref[: out_ref.shape[0], :] = start_ref[...]
+    total_ref[out_ref.shape[0] :, :] = jnp.zeros((edge, out_ref.shape[1]), jnp.float32)
+    live = late_ref[3, 0]
     together = math.gcd(slots, 12)
 
     def step(number, carry):
         products, places = [], []
         for inner in range(together):
-            slot = number * together + inner
-            block = pl.ds(pl.multiple_of(cols_ref[slot] * edge, edge), edge)
-            places.append(jnp.where(slot < live, rows_ref[slot], spare))
+            entry = number * together + inner
+            places.append(jnp.where(entry < live, late_ref[1, entry], spare))
             products.append(
-                jnp.dot(values_ref[slot], extended_ref[block, :], preferred_element_type=jnp.float32)
+                jnp.dot(
+                    values_ref[late_ref[0, entry]], extended_ref[late_ref[2, entry]],
+                    preferred_element_type=jnp.float32,
+                )
             )
         for place, product in zip(places, products):
             total_ref[pl.ds(pl.multiple_of(place * edge, edge), edge), :] += product
@@ -403,25 +511,40 @@
     hub_total = hub_ids.shape[0]
     edge = tile_values.shape[1]
     vmem = pl.BlockSpec(memory_space=pltpu.VMEM)
-    extended_rows = vertex_rows + slots * half_rows + hub_total
-    extended = pl.pallas_call(
+    blocks = (vertex_rows + slots * half_rows + hub_total) // edge
+    tile_slots = tile_values.shape[0]
+    hbm = pl.BlockSpec(memory_space=pltpu.HBM)
+    smem = pl.BlockSpec(memory_space=pltpu.SMEM)
+    extended, values, early_total, late = pl.pallas_call(
         functools.partial(exchange_kernel, count),
-        out_shape=jax.ShapeDtypeStruct((extended_rows, width), jnp.bfloat16),
-        in_specs=[pl.BlockSpec(memory_space=pltpu.HBM)] * 4,
-        out_specs=vmem,
+        out_shape=[
+            jax.ShapeDtypeStruct((blocks, edge, width), jnp.bfloat16),
+            jax.ShapeDtypeStruct(tile_values.shape, jnp.bfloat16),
+            jax.ShapeDtypeStruct((vertex_rows, width), jnp.float32),
+            pltpu.SMEM((8, tile_slots), jnp.int32),
+        ],
+        in_specs=[hbm] * 7 + [smem],
+        out_specs=[vmem] * 3 + [smem],
         scratch_shapes=[
             pltpu.VMEM((depth, vertex_rows), jnp.bfloat16),
             pltpu.VMEM(weight.shape, jnp.bfloat16),
             pltpu.VMEM((slots, half_rows), jnp.int32),
             pltpu.VMEM((1, hub_total), jnp.int32),
-            pltpu.SemaphoreType.DMA((4,)),
+            pltpu.VMEM((1, tile_slots), jnp.int32),
+            pltpu.VMEM((1, tile_slots), jnp.int32),
+            pltpu.SemaphoreType.DMA((8 + GROUPS,)),
+            pltpu.VMEM((blocks, edge, width), jnp.bfloat16),
+            pltpu.VMEM((8, tile_slots), jnp.int32),
+            pltpu.VMEM((8, tile_slots), jnp.int32),
+            pltpu.SMEM((8, tile_slots), jnp.int32),
+            pltpu.VMEM((tile_slots, edge, width), jnp.float32),
             pltpu.VMEM((width, vertex_rows), jnp.float32),
             pltpu.VMEM((width, vertex_rows), jnp.float32),
             pltpu.VMEM((width, vertex_rows), jnp.float32),
             pltpu.VMEM((vertex_rows // GROUPS, GROUPS * width), jnp.bfloat16),
             pltpu.VMEM((slots, half_rows), jnp.int32),
             pltpu.VMEM((half_rows, slots), jnp.int32),
-            pltpu.VMEM((slots, half_rows, width), jnp.bfloat16),
+            pltpu.VMEM((slots, half_rows // edge, edge, width), jnp.bfloat16),
             pltpu.VMEM((HUB_MOST, width), jnp.bfloat16),
             pltpu.VMEM((count * HUB_MOST, width), jnp.bfloat16),
             pltpu.VMEM((hub_total, width), jnp.bfloat16),
@@ -438,29 +561,23 @@
     )(
         *[
             pltpu.with_memory_space_constraint(value, pltpu.HBM)
-            for value in (jnp.transpose(features), weight, send_rows[0], hub_ids[None, :])
-        ]
+            for value in (
+                jnp.transpose(features), weight, send_rows[0], hub_ids[None, :],
+                tile_rows[None, :], tile_cols[None, :], tile_values,
+            )
+        ],
+        tile_count,
     )
     return pl.pallas_call(
         tiles_kernel,
         out_shape=jax.ShapeDtypeStruct((vertex_rows, width), jnp.bfloat16),
-        in_specs=[vmem] * 2 + [pl.BlockSpec(memory_space=pltpu.SMEM)] + [vmem] * 3,
+        in_specs=[smem] + [vmem] * 4,
         out_specs=vmem,
         scratch_shapes=[
             pltpu.VMEM((vertex_rows + edge, width), jnp.float32),
-            pltpu.SMEM(tile_rows.shape, jnp.int32),
-            pltpu.SMEM(tile_cols.shape, jnp.int32),
-            pltpu.SemaphoreType.DMA((2,)),
         ],
         compiler_params=pltpu.CompilerParams(vmem_limit_bytes=24 << 20),
-    )(
-        tile_rows,
-        tile_cols,
-        tile_count,
-        tile_values,
-        extended,
-        out_bias[None, :],
-    )
+    )(late, values, extended, early_total, out_bias[None, :])
 
 
 def solution(mesh):
@@ -479,7 +596,11 @@
 
     def program(features, weight, out_bias, *rest):
         whole_lanes = out_bias.shape[0] % (LANES * mesh.shape["feat"]) == 0
+        tile_values, send_rows, hub_ids = rest[0], rest[4], rest[5]
+        edge = tile_values.shape[1]
         fits = mesh.shape["feat"] == 2 and mesh.shape["dom"] % PLANE == 0
+        fits = fits and features.shape[0] % (mesh.shape["dom"] * GROUPS * edge) == 0
+        fits = fits and send_rows.shape[2] % (PIECES * edge) == 0 and hub_ids.shape[0] % edge == 0
         body = local if fits and whole_lanes else local_any
         return jax.shard_map(
             body, mesh=mesh, in_specs=in_specs, out_specs=out_specs, check_vma=False

time: 40.1 us -> 38.1 us (0.950)
  the two profiles are of different devices: /device:TPU:21 before, /device:TPU:0 now
where the time goes in v2:
time: 38.1 us; the launch traced here: 38 us
  Pallas kernels  37.3 us (98%)
  between operations  0.68 us (2%)
    pallas_call x1, Pallas kernels, local(): pl.pallas_call(functools.partial(exchange_kernel, count), out_shape=[jax....  35.8 us
    pallas_call x1, Pallas kernels, local(): pl.pallas_call(tiles_kernel, out_shape=jax.ShapeDtypeStruct((vertex_rows,...  1.51 us

profile of v2, /device:TPU:0, one launch (start us, length us, event | category | flops | bytes accessed | tf_op | source)
XLA Modules:
  0.0 38.0 jit_solution(11139203865028895429)
XLA Ops:
  0.0 0.0 copy-start
  0.7 35.8 %shard_map.91 = (bf16[82,128,128]{2,1,0:T(8,128)(2,1)S(1)}, bf16[108,128,128]{2,1,0:T(8,128)(2,1)S(1)}, f32[2048,128]{1,0:T(8,128)S(1)}, s32[8,108]{1,0:T(8,128)S(4)}) custom-call(bf16[304,2048]{1,0:T(8,128)(2,1)} %bitcast.7, bf16[608,256]{1,0:T(8,128)(2,1)} %weight_hbm.1, s32[8,1024]{1,0:T(8,128)} %bitcast.8, s32[1,256]{1,0:T(1,128)} %bitcast.9, ...), custom_call_target="tpu_custom_call" | custom-call | tf_op jit(solution)/shard_map/pallas_call | solution.py:518
  36.4 0.0 copy-done
  36.4 1.5 %shard_map.92 = bf16[2048,128]{1,0:T(8,128)(2,1)} custom-call(s32[8,108]{1,0:T(8,128)S(4)} %get-tuple-element.9.late_ref, bf16[108,128,128]{2,1,0:T(8,128)(2,1)S(1)} %get-tuple-element.10.values_ref, bf16[82,128,128]{2,1,0:T(8,128)(2,1)S(1)} %get-tuple-element.11.extended_ref, f32[2048,128]{1,0:T(8,128)S(1)} %get-tuple-element.12.start_ref, f32[1,128]{1,0:T(1,128)S(1)} %bitcast.6), custom_call_target="tpu_custom_call" | custom-call | tf_op jit(solution)/shard_map/pallas_call | solution.py:571
Async XLA Ops:
  0.0 36.4 %copy-start = (f32[128]{0:T(128)S(1)}, f32[128]{0:T(128)}, u32[]{:S(2)}) copy-start(f32[128]{0:T(128)} %param.11) | copy-start | bytes 1540

commit v3 on v2

--- a/solution.py
+++ b/solution.py
@@ -248,7 +248,7 @@
         loads[1 + group].wait()
         partial_ref[:, rows] = over_rows(
             weight_ref[own_depth, other_columns], features_ref[:, rows]
-        )
+        ).astype(jnp.bfloat16)
         if group == 0:
             pl.semaphore_wait(barrier, greeted)
         exchanges.append(
@@ -396,7 +396,7 @@
     send(5)
     gate(3)
     gate(4)
-    send(6, pieces=range(PIECES - 1))
+    send(6)
     send(7)
     hub_copy(0, across_place * lines, lines, across).wait_recv()
     pair_rows = 2 * lines * HUB_MOST
@@ -415,7 +415,6 @@
         device_id=(far, feat), device_id_type=MESH,
     )
     hub_exchange.start()
-    send(6, pieces=range(PIECES - 1, PIECES))
 
     for slot, offset in enumerate(offsets):
 
@@ -538,8 +537,8 @@
             pltpu.VMEM((8, tile_slots), jnp.int32),
             pltpu.SMEM((8, tile_slots), jnp.int32),
             pltpu.VMEM((tile_slots, edge, width), jnp.float32),
-            pltpu.VMEM((width, vertex_rows), jnp.float32),
-            pltpu.VMEM((width, vertex_rows), jnp.float32),
+            pltpu.VMEM((width, vertex_rows), jnp.bfloat16),
+            pltpu.VMEM((width, vertex_rows), jnp.bfloat16),
             pltpu.VMEM((width, vertex_rows), jnp.float32),
             pltpu.VMEM((vertex_rows // GROUPS, GROUPS * width), jnp.bfloat16),
             pltpu.VMEM((slots, half_rows), jnp.int32),

time: 38.1 us -> 37.4 us (0.982)
  Pallas kernels: 37.3 us -> 36.3 us
    pallas_call x1, Pallas kernels: 35.8 us -> 34.8 us  [local(): pl.pallas_call(functools.partial(exchange_kernel, count), out_shape=[jax....]
where the time goes in v3:
time: 37.4 us; the launch traced here: 37 us
  Pallas kernels  36.3 us (97%)
  between operations  0.68 us (2%)
    pallas_call x1, Pallas kernels, local(): pl.pallas_call(functools.partial(exchange_kernel, count), out_shape=[jax....  34.8 us
    pallas_call x1, Pallas kernels, local(): pl.pallas_call(tiles_kernel, out_shape=jax.ShapeDtypeStruct((vertex_rows,...  1.5 us

profile of v3, /device:TPU:0, one launch (start us, length us, event | category | flops | bytes accessed | tf_op | source)
XLA Modules:
  0.0 37.0 jit_solution(1116769583492349909)
XLA Ops:
  0.0 0.0 copy-start
  0.7 34.8 %shard_map.91 = (bf16[82,128,128]{2,1,0:T(8,128)(2,1)S(1)}, bf16[108,128,128]{2,1,0:T(8,128)(2,1)S(1)}, f32[2048,128]{1,0:T(8,128)S(1)}, s32[8,108]{1,0:T(8,128)S(4)}) custom-call(bf16[304,2048]{1,0:T(8,128)(2,1)} %bitcast.7, bf16[608,256]{1,0:T(8,128)(2,1)} %weight_hbm.1, s32[8,1024]{1,0:T(8,128)} %bitcast.8, s32[1,256]{1,0:T(1,128)} %bitcast.9, ...), custom_call_target="tpu_custom_call" | custom-call | tf_op jit(solution)/shard_map/pallas_call | solution.py:517
  35.5 0.0 copy-done
  35.5 1.5 %shard_map.92 = bf16[2048,128]{1,0:T(8,128)(2,1)} custom-call(s32[8,108]{1,0:T(8,128)S(4)} %get-tuple-element.9.late_ref, bf16[108,128,128]{2,1,0:T(8,128)(2,1)S(1)} %get-tuple-element.10.values_ref, bf16[82,128,128]{2,1,0:T(8,128)(2,1)S(1)} %get-tuple-element.11.extended_ref, f32[2048,128]{1,0:T(8,128)S(1)} %get-tuple-element.12.start_ref, f32[1,128]{1,0:T(1,128)S(1)} %bitcast.6), custom_call_target="tpu_custom_call" | custom-call | tf_op jit(solution)/shard_map/pallas_call | solution.py:570
Async XLA Ops:
  0.0 35.5 %copy-start = (f32[128]{0:T(128)S(1)}, f32[128]{0:T(128)}, u32[]{:S(2)}) copy-start(f32[128]{0:T(128)} %param.11) | copy-start | bytes 1540

commit v4 on v3

--- a/solution.py
+++ b/solution.py
@@ -249,8 +249,10 @@
         partial_ref[:, rows] = over_rows(
             weight_ref[own_depth, other_columns], features_ref[:, rows]
         ).astype(jnp.bfloat16)
-        if group == 0:
-            pl.semaphore_wait(barrier, greeted)
+
+    pl.semaphore_wait(barrier, greeted)
+
+    for group, rows in enumerate(feature_parts):
         exchanges.append(
             pltpu.make_async_remote_copy(
                 src_ref=partial_ref.at[:, rows], dst_ref=other_ref.at[:, rows],

time: 37.4 us -> 37.6 us (level); the launches traced: 37 us -> 37.6 us
  Pallas kernels: 36.3 us -> 36.9 us
where the time goes in v4:
time: 37.6 us
  Pallas kernels  36.9 us (98%)
  between operations  0.68 us (2%)
    pallas_call x1, Pallas kernels, local(): pl.pallas_call(functools.partial(exchange_kernel, count), out_shape=[jax....  35.1 us
    pallas_call x1, Pallas kernels, local(): pl.pallas_call(tiles_kernel, out_shape=jax.ShapeDtypeStruct((vertex_rows,...  1.77 us

profile of v4, /device:TPU:0, one launch (start us, length us, event | category | flops | bytes accessed | tf_op | source)
XLA Modules:
  0.0 37.6 jit_solution(11594742807918417210)
XLA Ops:
  0.0 0.0 copy-start
  0.7 35.1 %shard_map.91 = (bf16[82,128,128]{2,1,0:T(8,128)(2,1)S(1)}, bf16[108,128,128]{2,1,0:T(8,128)(2,1)S(1)}, f32[2048,128]{1,0:T(8,128)S(1)}, s32[8,108]{1,0:T(8,128)S(4)}) custom-call(bf16[304,2048]{1,0:T(8,128)(2,1)} %bitcast.7, bf16[608,256]{1,0:T(8,128)(2,1)} %weight_hbm.1, s32[8,1024]{1,0:T(8,128)} %bitcast.8, s32[1,256]{1,0:T(1,128)} %bitcast.9, ...), custom_call_target="tpu_custom_call" | custom-call | tf_op jit(solution)/shard_map/pallas_call | solution.py:519
  35.8 0.0 copy-done
  35.8 1.8 %shard_map.92 = bf16[2048,128]{1,0:T(8,128)(2,1)} custom-call(s32[8,108]{1,0:T(8,128)S(4)} %get-tuple-element.9.late_ref, bf16[108,128,128]{2,1,0:T(8,128)(2,1)S(1)} %get-tuple-element.10.values_ref, bf16[82,128,128]{2,1,0:T(8,128)(2,1)S(1)} %get-tuple-element.11.extended_ref, f32[2048,128]{1,0:T(8,128)S(1)} %get-tuple-element.12.start_ref, f32[1,128]{1,0:T(1,128)S(1)} %bitcast.6), custom_call_target="tpu_custom_call" | custom-call | tf_op jit(solution)/shard_map/pallas_call | solution.py:572
Async XLA Ops:
  0.0 35.8 %copy-start = (f32[128]{0:T(128)S(1)}, f32[128]{0:T(128)}, u32[]{:S(2)}) copy-start(f32[128]{0:T(128)} %param.11) | copy-start | bytes 1540
